TPU v7x, 128 devices: a whole 4x4x4 slice. The times are simulated.
128 devices in a mesh: row: 8 (over y, core), col: 16 (over x, z).
Axes of the slice: x: 4, y: 4, z: 4, core: 2. Of those that a mesh axis runs over, the one named last changes fastest.
Arguments:
- matrix_in: float32 [4, 4096, 2, 8192], P(None, 'row', None, 'col'), as said below
- panel_start: int32 [1], replicated, may hold values from 0 to 29
Outputs:
- matrix_out: float32 [4, 4096, 2, 8192], P(None, 'row', None, 'col')
Inputs may be any that keep to these rules, and one draw needn't show every extreme that they name: matrix_in is symmetric and positive definite.
All inputs are finite; a program needn't handle non-finite values.
Results may differ from a plain program's by a relative error of at most 0.0001.
Values sent between devices are 32-bit elements.
No kernel may reach another device: no remote copies, remote signals or barrier semaphores. Data moves between devices by JAX's collectives and lax.ppermute only.
A program may use at most 128 MiB of HBM per device.

v0:
```python
import jax
import jax.numpy as jnp
from jax import lax
from jax.sharding import PartitionSpec as P


def picked(x, axis, root):
    return lax.dynamic_index_in_dim(lax.all_gather(x, axis), root, 0, keepdims=False)


def from_root(value, axis, source):
    kept = jnp.where(lax.axis_index(axis) == source, value, 0).astype(value.dtype)
    return lax.psum(kept, axis)


def padded_to(lines, length):
    spare = -lines.shape[0] % length
    if not spare:
        return lines
    return jnp.concatenate([lines, jnp.zeros((spare, *lines.shape[1:]), lines.dtype)])


def broadcast_by_parts(x, axis, root):
    lines = jnp.where(lax.axis_index(axis) == root, x, jnp.zeros_like(x)).reshape(
        -1, *x.shape[1:][-1:]
    )
    padded = padded_to(lines, lax.axis_size(axis))
    own = lax.psum_scatter(padded, axis, scatter_dimension=0, tiled=True)
    return lax.all_gather(own, axis, axis=0, tiled=True)[: len(lines)].reshape(x.shape)


def update(matrix, rows_part, cols_part):
    loc_rows, width, _unused_a = rows_part.shape
    loc_cols = cols_part.shape[0]
    left_panel = rows_part.reshape(loc_rows * width, width)
    right_panel = cols_part.reshape(loc_cols * width, width)
    product = lax.dot_general(
        left_panel,
        right_panel,
        (((1,), (1,)), ((), ())),
        precision=lax.Precision.HIGHEST,
        preferred_element_type=jnp.float32,
    )
    return matrix - product.reshape(loc_rows, width, loc_cols, width)


def factor_panel(matrix, panel):
    rows_dev = lax.axis_size("row")
    cols_dev = lax.axis_size("col")
    my_row = lax.axis_index("row")
    my_col = lax.axis_index("col")
    loc_rows, width, loc_cols, _unused_b = matrix.shape
    row_blocks = jnp.arange(loc_rows, dtype=jnp.int32) * rows_dev + my_row
    col_local = panel // cols_dev
    row_local = panel // rows_dev
    owner_row = panel % rows_dev
    owner_col = panel % cols_dev
    column_strip = lax.dynamic_index_in_dim(matrix, col_local, 2, keepdims=False)
    diag_raw = lax.dynamic_index_in_dim(column_strip, row_local, 0, keepdims=False)
    factor = picked(jnp.linalg.cholesky(diag_raw), "row", owner_row)
    flat_rows = column_strip.reshape(loc_rows * width, width)
    solved = jax.scipy.linalg.solve_triangular(factor, flat_rows.T, lower=True).T
    solved = solved.reshape(loc_rows, width, width)
    below_panel = (row_blocks > panel)[:, None, None]
    on_panel = (row_blocks == panel)[:, None, None]
    rows_local = jnp.where(below_panel, solved, jnp.float32(0.0))
    rows_part = from_root(rows_local, "col", owner_col)
    new_strip = jnp.where(below_panel, solved, column_strip)
    new_strip = jnp.where(on_panel, factor[None, :, :], new_strip)
    written = jnp.where(my_col == owner_col, new_strip, column_strip)
    matrix = lax.dynamic_update_index_in_dim(matrix, written, col_local, 2)
    stride_ratio = cols_dev // rows_dev
    source_row = my_col % rows_dev
    offset_pick = my_col // rows_dev
    received = broadcast_by_parts(rows_part, "row", source_row)
    grouped = received.reshape(loc_cols, stride_ratio, width, width)
    cols_part = lax.dynamic_index_in_dim(grouped, offset_pick, 1, keepdims=False)
    return (rows_part, cols_part, matrix)


def per_device(matrix_in, panel_start):
    first_panel = panel_start[0]
    matrix = matrix_in
    cols_dev = lax.axis_size("col")
    loc_rows, width, loc_cols, _unused_c = matrix.shape
    rows_first, cols_first, matrix = factor_panel(matrix, first_panel)
    next_panel = first_panel + 1
    col_next = next_panel // cols_dev
    next_strip = lax.dynamic_index_in_dim(matrix, col_next, 2, keepdims=False)
    next_piece = lax.dynamic_index_in_dim(cols_first, col_next, 0, keepdims=False)
    left_panel = rows_first.reshape(loc_rows * width, width)
    strip_product = lax.dot_general(
        left_panel,
        next_piece,
        (((1,), (1,)), ((), ())),
        precision=lax.Precision.HIGHEST,
        preferred_element_type=jnp.float32,
    )
    next_strip = next_strip - strip_product.reshape(loc_rows, width, width)
    matrix = lax.dynamic_update_index_in_dim(matrix, next_strip, col_next, 2)
    rows_second, cols_second, matrix = factor_panel(matrix, next_panel)
    skipped = (jnp.arange(loc_cols, dtype=jnp.int32) == col_next)[:, None, None]
    cols_rest = jnp.where(skipped, jnp.float32(0.0), cols_first)
    matrix = update(matrix, rows_first, cols_rest)
    matrix = update(matrix, rows_second, cols_second)
    return matrix


def solution(mesh):
    return jax.shard_map(
        per_device,
        mesh=mesh,
        in_specs=(P(None, "row", None, "col"), P()),
        out_specs=P(None, "row", None, "col"),
        check_vma=False,
    )
```

profile of v0, /device:TPU:1, one launch (start us, length us, event | category | flops | bytes accessed | tf_op | source)
XLA Modules:
  0.0 873.0 jit_solution(14277893120988400959)
XLA Ops:
  11.3 11.7 %cholesky.286 = f32[128,128]{1,0:T(8,128)S(1)} custom-call(f32[128,128]{1,0:T(8,128)S(1)} %cholesky.426), custom_call_target="Cholesky" | custom-call | tf_op jit(solution)/shard_map/jit(cholesky)/cholesky | solution.py:60
  33.7 11.7 %cholesky.305 = f32[128,128]{1,0:T(8,128)S(1)} custom-call(f32[128,128]{1,0:T(8,128)S(1)} %cholesky.430), custom_call_target="Cholesky" | custom-call | tf_op jit(solution)/shard_map/jit(cholesky)/cholesky | solution.py:60
  45.4 10.0 %custom-call.28 = f32[1,128,128]{1,2,0:T(8,128)S(1)} custom-call(f32[1,128,128]{2,1,0:T(8,128)S(1)} %get-tuple-element.63), custom_call_target="InvertDiagBlocksLowerTriangular" | custom-call | tf_op jit(solution)/shard_map/jit(cholesky)/cholesky | solution.py:60
  56.1 11.7 %cholesky.326 = f32[128,128]{1,0:T(8,128)S(1)} custom-call(f32[128,128]{1,0:T(8,128)S(1)} %cholesky.435), custom_call_target="Cholesky" | custom-call | tf_op jit(solution)/shard_map/jit(cholesky)/cholesky | solution.py:60
  78.9 11.7 %cholesky.343 = f32[128,128]{1,0:T(8,128)S(1)} custom-call(f32[128,128]{1,0:T(8,128)S(1)} %convolution_subtract_fusion.9), custom_call_target="Cholesky" | custom-call | tf_op jit(solution)/shard_map/jit(cholesky)/cholesky | solution.py:60
  109.0 40.4 %all-gather.11.cloned.1.call-done = f32[4096,512]{1,0:T(8,128)} async-done(((f32[512,512]{1,0:T(8,128)}), f32[4096,512]{1,0:T(8,128)}) %all-gather.11.cloned.1.call-update) | async-done | bytes 8388624 | tf_op jit(solution)/shard_map/all_gather | solution.py:8
  159.2 39.7 %custom-call.30 = f32[4,128,128]{1,2,0:T(8,128)S(1)} custom-call(f32[4,128,128]{2,1,0:T(8,128)S(1)} %get-tuple-element.21), custom_call_target="InvertDiagBlocksLowerTriangular" | custom-call | tf_op jit(solution)/shard_map/jit(_solve_triangular)/triangular_solve | solution.py:62
  229.5 103.3 %all-reduce.4.cloned.1.call-done = f32[4,512,512]{2,1,0:T(8,128)} async-done(((f32[4,512,512]{2,1,0:T(8,128)}), f32[4,512,512]{2,1,0:T(8,128)}) %all-reduce.4.cloned.1.call-update) | async-done | bytes 4194320 | tf_op jit(solution)/shard_map/psum | solution.py:13
  335.3 36.9 %reduce-scatter.3.cloned.1.call-done = f32[256,512]{1,0:T(8,128)} async-done(((f32[2048,512]{1,0:T(8,128)}), f32[256,512]{1,0:T(8,128)}) %reduce-scatter.3.cloned.1.call-update) | async-done | bytes 524304 | tf_op jit(solution)/shard_map/reduce_scatter | solution.py:28
  383.7 24.3 %all-gather.7.cloned.1.call-done = f32[2048,512]{1,0:T(8,128)} async-done(((f32[256,512]{1,0:T(8,128)}), f32[2048,512]{1,0:T(8,128)}) %all-gather.7.cloned.1.call-update) | async-done | bytes 4194320 | tf_op jit(solution)/shard_map/all_gather | solution.py:29
  408.0 11.0 %bitcast_dynamic-update-slice_fusion.2 = f32[4,512,2,512]{3,1,2,0:T(8,128)} fusion(f32[4,512,2,512]{3,1,2,0:T(8,128)} %select_dynamic-update-slice_fusion.1, s32[]{:T(128)S(6)} %select_n.178, f32[4,512,1,512]{3,1,2,0:T(8,128)} %constant_dynamic-slice_fusion.4, f32[4,512,512]{2,1,0:T(8,128)} %all-reduce.4.cloned.1.call-done, ...), kind=kOutput, calls=%fused_computation.11 | convolution fusion | flops 6443499520 | bytes 13631500 | tf_op jit(solution)/shard_map/dot_general | solution.py:92
  422.1 11.7 %cholesky.358 = f32[128,128]{1,0:T(8,128)S(1)} custom-call(f32[128,128]{1,0:T(8,128)S(1)} %cholesky.439), custom_call_target="Cholesky" | custom-call | tf_op jit(solution)/shard_map/jit(cholesky)/cholesky | solution.py:60
  445.1 11.7 %cholesky.377 = f32[128,128]{1,0:T(8,128)S(1)} custom-call(f32[128,128]{1,0:T(8,128)S(1)} %cholesky.443), custom_call_target="Cholesky" | custom-call | tf_op jit(solution)/shard_map/jit(cholesky)/cholesky | solution.py:60
  457.6 10.2 %custom-call.32 = f32[1,128,128]{1,2,0:T(8,128)S(1)} custom-call(f32[1,128,128]{2,1,0:T(8,128)S(1)} %get-tuple-element.53), custom_call_target="InvertDiagBlocksLowerTriangular" | custom-call | tf_op jit(solution)/shard_map/jit(cholesky)/cholesky | solution.py:60
  468.5 11.7 %cholesky.398 = f32[128,128]{1,0:T(8,128)S(1)} custom-call(f32[128,128]{1,0:T(8,128)S(1)} %cholesky.448), custom_call_target="Cholesky" | custom-call | tf_op jit(solution)/shard_map/jit(cholesky)/cholesky | solution.py:60
  491.3 11.7 %cholesky.415 = f32[128,128]{1,0:T(8,128)S(1)} custom-call(f32[128,128]{1,0:T(8,128)S(1)} %convolution_subtract_fusion.8), custom_call_target="Cholesky" | custom-call | tf_op jit(solution)/shard_map/jit(cholesky)/cholesky | solution.py:60
  512.2 45.1 %all-gather.13.cloned.1.call-done = f32[4096,512]{1,0:T(8,128)} async-done(((f32[512,512]{1,0:T(8,128)}), f32[4096,512]{1,0:T(8,128)}) %all-gather.13.cloned.1.call-update) | async-done | bytes 8388624 | tf_op jit(solution)/shard_map/all_gather | solution.py:8
  566.7 39.3 %custom-call.34 = f32[4,128,128]{1,2,0:T(8,128)S(1)} custom-call(f32[4,128,128]{2,1,0:T(8,128)S(1)} %get-tuple-element.22), custom_call_target="InvertDiagBlocksLowerTriangular" | custom-call | tf_op jit(solution)/shard_map/jit(_solve_triangular)/triangular_solve | solution.py:62
  636.8 103.3 %all-reduce.6.cloned.1.call-done = f32[4,512,512]{2,1,0:T(8,128)} async-done(((f32[4,512,512]{2,1,0:T(8,128)}), f32[4,512,512]{2,1,0:T(8,128)}) %all-reduce.6.cloned.1.call-update) | async-done | bytes 4194320 | tf_op jit(solution)/shard_map/psum | solution.py:13
  742.6 36.9 %reduce-scatter.5.cloned.1.call-done = f32[256,512]{1,0:T(8,128)} async-done(((f32[2048,512]{1,0:T(8,128)}), f32[256,512]{1,0:T(8,128)}) %reduce-scatter.5.cloned.1.call-update) | async-done | bytes 524304 | tf_op jit(solution)/shard_map/reduce_scatter | solution.py:28
  786.3 29.1 %all-gather.9.cloned.1.call-done = f32[2048,512]{1,0:T(8,128)} async-done(((f32[256,512]{1,0:T(8,128)}), f32[2048,512]{1,0:T(8,128)}) %all-gather.9.cloned.1.call-update) | async-done | bytes 4194320 | tf_op jit(solution)/shard_map/all_gather | solution.py:29
  815.5 17.0 %fusion = f32[4,512,2,512]{3,1,2,0:T(8,128)S(1)} fusion(f32[4,512,512]{2,1,0:T(8,128)} %all-reduce.6.cloned.1.call-done, f32[2,2,512,512]{3,2,1,0:T(8,128)} %bitcast.194, s32[]{:T(128)S(6)} %select_n.187), kind=kOutput, calls=%fused_computation.7 | convolution fusion | flops 12884901888 | bytes 14680068 | tf_op jit(solution)/shard_map/dot_general | solution.py:37
  832.5 18.1 %subtract_subtract_fusion = f32[4,512,2,512]{3,1,2,0:T(8,128)} fusion(f32[4,512,2,512]{3,1,2,0:T(8,128)S(1)} %fusion, f32[4,512,2,512]{3,1,2,0:T(8,128)S(1)} %copy-done, f32[4,512,512]{2,1,0:T(8,128)S(1)} %copy-done.1, f32[2,2,512,512]{3,2,1,0:T(8,128)} %bitcast.193, s32[]{:T(128)S(6)} %select_n.187, pred[2]{0:T(512)(128)(4,1)S(1)} %iota_compare_fusion.3), kind=kOutput, calls=%fused_computation.4 | convolution fusion | flops 12889620480 | bytes 31457286 | tf_op jit(solution)/shard_map/dot_general | solution.py:37
  850.6 15.4 %copy.15 = f32[4,512,2,512]{3,2,1,0:T(2,128)} copy(f32[4,512,2,512]{3,1,2,0:T(8,128)} %subtract_subtract_fusion) | data formatting | bytes 16777216 | tf_op jit(solution)/shard_map/sub | solution.py:44
  (135 shorter events, 195.1 us)
Async XLA Ops:
  6.5 142.9 %all-gather.11.cloned.1.call-start = ((), (), s32[]{:S(2)}) async-start(), calls=%async_computation.8 | async-start | bytes 9437184 | tf_op jit(solution)/shard_map/all_gather | solution.py:8
  96.0 236.8 %all-reduce.4.cloned.1.call-start = ((), (), s32[]{:S(2)}) async-start(), calls=%async_computation.2 | async-start | bytes 8388608 | tf_op jit(solution)/shard_map/psum | solution.py:13
  198.9 6.6 copy-start.3
  229.4 142.7 %reduce-scatter.3.cloned.1.call-start = ((), (), s32[]{:S(2)}) async-start(), calls=%async_computation.3 | async-start | bytes 4718592 | tf_op jit(solution)/shard_map/reduce_scatter | solution.py:28
  335.3 72.8 %all-gather.7.cloned.1.call-start = ((), (), s32[]{:S(2)}) async-start(), calls=%async_computation.4 | async-start | bytes 4718592 | tf_op jit(solution)/shard_map/all_gather | solution.py:29
  372.2 185.1 %all-gather.13.cloned.1.call-start = ((), (), s32[]{:S(2)}) async-start(), calls=%async_computation.9 | async-start | bytes 9437184 | tf_op jit(solution)/shard_map/all_gather | solution.py:8
  507.6 232.5 %all-reduce.6.cloned.1.call-start = ((), (), s32[]{:S(2)}) async-start(), calls=%async_computation.5 | async-start | bytes 8388608 | tf_op jit(solution)/shard_map/psum | solution.py:13
  606.0 6.6 copy-start.2
  636.8 142.7 %reduce-scatter.5.cloned.1.call-start = ((), (), s32[]{:S(2)}) async-start(), calls=%async_computation.6 | async-start | bytes 4718592 | tf_op jit(solution)/shard_map/reduce_scatter | solution.py:28
  742.5 72.9 %all-gather.9.cloned.1.call-start = ((), (), s32[]{:S(2)}) async-start(), calls=%async_computation.7 | async-start | bytes 4718592 | tf_op jit(solution)/shard_map/all_gather | solution.py:29
  815.5 17.0 %copy-start = (f32[4,512,2,512]{3,1,2,0:T(8,128)S(1)}, f32[4,512,2,512]{3,1,2,0:T(8,128)}, u32[]{:S(2)}) copy-start(f32[4,512,2,512]{3,1,2,0:T(8,128)} %select_dynamic-update-slice_fusion) | copy-start | bytes 25165828
  815.5 17.0 %copy-start.1 = (f32[4,512,512]{2,1,0:T(8,128)S(1)}, f32[4,512,512]{2,1,0:T(8,128)}, u32[]{:S(2)}) copy-start(f32[4,512,512]{2,1,0:T(8,128)} %all-reduce.4.cloned.1.call-done) | copy-start | bytes 12582916
Sparse Core Ops, SparseCore 0:
  96.1 53.2 all-gather.10
  229.5 103.1 all-reduce.3
  335.4 36.7 reduce-scatter.2
  373.7 34.2 all-gather.6
  507.7 49.6 all-gather.12
  636.9 103.1 all-reduce.5
  742.7 36.7 reduce-scatter.4
  781.2 34.2 all-gather.8
where the time goes:
time: 883 us; the launch traced here: 873 us
  waiting for transfers between devices  419 us (47%)
  other arithmetic  278 us (31%)
  matrix products  85.5 us (10%)
  local copies, waits for them, and re-layouts  69.8 us (8%)
  between operations  20.2 us (2%)
    psum x2, waiting for transfers between devices, from_root(): return lax.psum(kept, axis)  207 us
    another operation x29, other arithmetic, factor_panel(): factor = picked(jnp.linalg.cholesky(diag_raw), 'row', owner_row)  158 us
    all_gather x2, waiting for transfers between devices, picked(): lax.all_gather(x, axis)  85.5 us
    another operation x5, other arithmetic, factor_panel(): jax.scipy.linalg.solve_triangular(factor, flat_rows.T, lower=True)  82 us
    reduce_scatter x2, waiting for transfers between devices, broadcast_by_parts(): own = lax.psum_scatter(padded, axis, scatter_dimension=0, tiled=True)  73.7 us
    all_gather x2, waiting for transfers between devices, broadcast_by_parts(): lax.all_gather(own, axis, axis=0, tiled=True)[:len(lines)].reshape(x.shape)  53.5 us
    another operation x14, matrix products, factor_panel(): jax.scipy.linalg.solve_triangular(factor, flat_rows.T, lower=True)  35.7 us
    dot_general x2, matrix products, update(): lax.dot_general(left_panel, right_panel, (((1,), (1,)), ((), ())), precis...  35.1 us
  transfers between devices with their start and end apart: 8, of which 8 were waited for; matrix products, arithmetic and copies ran while one was open for 4% of the time, Pallas kernels for 0%

commit v1 on v0

--- a/solution.py
+++ b/solution.py
@@ -10,7 +10,7 @@
 
 def from_root(value, axis, source):
     kept = jnp.where(lax.axis_index(axis) == source, value, 0).astype(value.dtype)
-    return lax.psum(kept, axis)
+    return jnp.sum(lax.all_gather(kept, axis), axis=0)
 
 
 def padded_to(lines, length):

time: 883 us -> 1500 us (1.70)
  waiting for transfers between devices: 419 us -> 937 us
  other arithmetic: 278 us -> 322 us
  local copies, waits for them, and re-layouts: 69.8 us -> 107 us
    all_gather x0 -> x2, waiting for transfers between devices: none -> 737 us  [from_root(): return jnp.sum(lax.all_gather(kept, axis), axis=0)]
    psum x2 -> x0, waiting for transfers between devices: 207 us -> none  [from_root(): return lax.psum(kept, axis)]
    reduce_sum x0 -> x2, other arithmetic: none -> 46.2 us  [from_root(): return jnp.sum(lax.all_gather(kept, axis), axis=0)]
    dot_general x2, matrix products: 35.1 us -> 62.2 us  [update(): lax.dot_general(left_panel, right_panel, (((1,), (1,)), ((), ())), precis...]
  transfers between devices with their start and end apart: 8 -> 8, of which waited for: 8 -> 8; matrix products, arithmetic and copies ran while one was open for 4% -> 3% of each run, Pallas kernels for 0% -> 0%
where the time goes in v1:
time: 1500 us; the launch traced here: 1490 us
  waiting for transfers between devices  937 us (62%)
  other arithmetic  322 us (21%)
  local copies, waits for them, and re-layouts  107 us (7%)
  matrix products  99.1 us (7%)
  between operations  20.1 us (1%)
    all_gather x2, waiting for transfers between devices, from_root(): return jnp.sum(lax.all_gather(kept, axis), axis=0)  737 us
    another operation x29, other arithmetic, factor_panel(): factor = picked(jnp.linalg.cholesky(diag_raw), 'row', owner_row)  158 us
    another operation x5, other arithmetic, factor_panel(): jax.scipy.linalg.solve_triangular(factor, flat_rows.T, lower=True)  81.6 us
    all_gather x2, waiting for transfers between devices, picked(): lax.all_gather(x, axis)  74.1 us
    reduce_scatter x2, waiting for transfers between devices, broadcast_by_parts(): own = lax.psum_scatter(padded, axis, scatter_dimension=0, tiled=True)  73.1 us
    dot_general x2, matrix products, update(): lax.dot_general(left_panel, right_panel, (((1,), (1,)), ((), ())), precis...  62.2 us
    all_gather x2, waiting for transfers between devices, broadcast_by_parts(): lax.all_gather(own, axis, axis=0, tiled=True)[:len(lines)].reshape(x.shape)  53.4 us
    reduce_sum x2, other arithmetic, from_root(): return jnp.sum(lax.all_gather(kept, axis), axis=0)  46.2 us
  transfers between devices with their start and end apart: 8, of which 8 were waited for; matrix products, arithmetic and copies ran while one was open for 3% of the time, Pallas kernels for 0%

profile of v1, /device:TPU:1, one launch (start us, length us, event | category | flops | bytes accessed | tf_op | source)
XLA Modules:
  0.0 1486.1 jit_solution(1432974212987800538)
XLA Ops:
  11.3 11.7 cholesky.286
  33.7 11.7 cholesky.305
  56.1 11.7 cholesky.326
  78.9 11.7 cholesky.343
  114.7 34.4 %all-gather.17.cloned.1.call-done = f32[4096,512]{1,0:T(8,128)} async-done(((f32[512,512]{1,0:T(8,128)}), f32[4096,512]{1,0:T(8,128)}) %all-gather.17.cloned.1.call-update) | async-done | bytes 8388624 | tf_op jit(solution)/shard_map/all_gather | solution.py:8
  158.8 39.3 %custom-call.30 = f32[4,128,128]{1,2,0:T(8,128)S(1)} custom-call(f32[4,128,128]{2,1,0:T(8,128)S(1)} %get-tuple-element.21), custom_call_target="InvertDiagBlocksLowerTriangular" | custom-call | tf_op jit(solution)/shard_map/jit(_solve_triangular)/triangular_solve | solution.py:62
  222.2 368.3 %all-gather.9.cloned.1.call-done = f32[16,4,512,512]{3,2,1,0:T(8,128)} async-done(((f32[1,4,512,512]{3,2,1,0:T(8,128)}), f32[16,4,512,512]{3,2,1,0:T(8,128)}) %all-gather.9.cloned.1.call-update) | async-done | bytes 67108880 | tf_op jit(solution)/shard_map/all_gather | solution.py:13
  590.6 23.1 %reduce_sum.18 = f32[4,512,512]{2,1,0:T(8,128)} reduce(f32[16,4,512,512]{3,2,1,0:T(8,128)} %all-gather.9.cloned.1.call-done, f32[]{:T(128)} %constant.302.clone.1), dimensions={0}, to_apply=%region_8.11 | reduce | flops 15728640 | bytes 71303168 | tf_op jit(solution)/shard_map/reduce_sum | solution.py:13
  623.9 36.5 %reduce-scatter.3.cloned.1.call-done = f32[256,512]{0,1:T(8,128)} async-done(((f32[2048,512]{0,1:T(8,128)}), f32[256,512]{0,1:T(8,128)}) %reduce-scatter.3.cloned.1.call-update) | async-done | bytes 524304 | tf_op jit(solution)/shard_map/reduce_scatter | solution.py:28
  672.1 24.2 %all-gather.11.cloned.1.call-done = f32[2048,512]{0,1:T(8,128)} async-done(((f32[256,512]{0,1:T(8,128)}), f32[2048,512]{0,1:T(8,128)}) %all-gather.11.cloned.1.call-update) | async-done | bytes 4194320 | tf_op jit(solution)/shard_map/all_gather | solution.py:29
  701.7 11.0 bitcast_dynamic-update-slice_fusion.2
  715.8 11.7 cholesky.358
  738.2 11.7 cholesky.377
  762.2 11.7 cholesky.398
  784.9 11.7 cholesky.415
  811.3 39.6 %all-gather.19.cloned.1.call-done = f32[4096,512]{1,0:T(8,128)} async-done(((f32[512,512]{1,0:T(8,128)}), f32[4096,512]{1,0:T(8,128)}) %all-gather.19.cloned.1.call-update) | async-done | bytes 8388624 | tf_op jit(solution)/shard_map/all_gather | solution.py:8
  860.5 39.3 %custom-call.34 = f32[4,128,128]{1,2,0:T(8,128)S(1)} custom-call(f32[4,128,128]{2,1,0:T(8,128)S(1)} %get-tuple-element.22), custom_call_target="InvertDiagBlocksLowerTriangular" | custom-call | tf_op jit(solution)/shard_map/jit(_solve_triangular)/triangular_solve | solution.py:62
  923.7 368.4 %all-gather.13.cloned.1.call-done = f32[16,4,512,512]{3,2,1,0:T(8,128)} async-done(((f32[1,4,512,512]{3,2,1,0:T(8,128)}), f32[16,4,512,512]{3,2,1,0:T(8,128)}) %all-gather.13.cloned.1.call-update) | async-done | bytes 67108880 | tf_op jit(solution)/shard_map/all_gather | solution.py:13
  1292.1 23.1 %reduce_sum.19 = f32[4,512,512]{2,1,0:T(8,128)} reduce(f32[16,4,512,512]{3,2,1,0:T(8,128)} %all-gather.13.cloned.1.call-done, f32[]{:T(128)} %constant.302.clone.1), dimensions={0}, to_apply=%region_10.13 | reduce | flops 15728640 | bytes 71303168 | tf_op jit(solution)/shard_map/reduce_sum | solution.py:13
  1328.8 36.5 %reduce-scatter.5.cloned.1.call-done = f32[256,512]{1,0:T(8,128)} async-done(((f32[2048,512]{1,0:T(8,128)}), f32[256,512]{1,0:T(8,128)}) %reduce-scatter.5.cloned.1.call-update) | async-done | bytes 524304 | tf_op jit(solution)/shard_map/reduce_scatter | solution.py:28
  1372.3 29.1 %all-gather.15.cloned.1.call-done = f32[2048,512]{1,0:T(8,128)} async-done(((f32[256,512]{1,0:T(8,128)}), f32[2048,512]{1,0:T(8,128)}) %all-gather.15.cloned.1.call-update) | async-done | bytes 4194320 | tf_op jit(solution)/shard_map/all_gather | solution.py:29
  1401.4 30.7 %fusion = f32[4,512,2,512]{3,1,2,0:T(8,128)S(1)} fusion(f32[4,512,512,1]{1,0,2,3:T(4,128)} %bitcast.168, f32[2,2,512,512]{3,2,1,0:T(8,128)} %bitcast.188, s32[]{:T(128)S(6)} %select_n.224), kind=kOutput, calls=%fused_computation.8 | convolution fusion | flops 12884901888 | bytes 14680068 | tf_op jit(solution)/shard_map/dot_general | solution.py:37
  1432.1 31.6 %subtract_subtract_fusion = f32[4,512,2,512]{3,1,2,0:T(8,128)} fusion(f32[4,512,2,512]{3,1,2,0:T(8,128)S(1)} %fusion, f32[4,512,2,512]{3,1,2,0:T(8,128)S(1)} %copy-done, f32[4,512,512,1]{1,0,2,3:T(4,128)S(1)} %bitcast.167, f32[2,2,512,512]{3,2,1,0:T(8,128)} %bitcast.187, s32[]{:T(128)S(6)} %select_n.224, pred[2]{0:T(512)(128)(4,1)S(1)} %iota_compare_fusion.3), kind=kOutput, calls=%fused_computation.4 | convolution fusion | flops 12889620480 | bytes 31457286 | tf_op jit(solution)/shard_map/dot_general | solution.py:37
  1463.7 15.4 %copy.43 = f32[4,512,2,512]{3,2,1,0:T(2,128)} copy(f32[4,512,2,512]{3,1,2,0:T(8,128)} %subtract_subtract_fusion) | data formatting | bytes 16777216 | tf_op jit(solution)/shard_map/sub | solution.py:44
  (144 shorter events, 237.8 us)
Async XLA Ops:
  6.5 142.6 %all-gather.17.cloned.1.call-start = ((), (), s32[]{:S(2)}) async-start(), calls=%async_computation.8 | async-start | bytes 9437184 | tf_op jit(solution)/shard_map/all_gather | solution.py:8
  95.7 494.9 %all-gather.9.cloned.1.call-start = ((), (), s32[]{:S(2)}) async-start(), calls=%async_computation.2 | async-start | bytes 71303168 | tf_op jit(solution)/shard_map/all_gather | solution.py:13
  198.2 5.7 copy-start.2
  222.2 438.3 %reduce-scatter.3.cloned.1.call-start = ((), (), s32[]{:S(2)}) async-start(), calls=%async_computation.3 | async-start | bytes 4718592 | tf_op jit(solution)/shard_map/reduce_scatter | solution.py:28
  623.9 72.4 %all-gather.11.cloned.1.call-start = ((), (), s32[]{:S(2)}) async-start(), calls=%async_computation.4 | async-start | bytes 4718592 | tf_op jit(solution)/shard_map/all_gather | solution.py:29
  660.5 190.4 %all-gather.19.cloned.1.call-start = ((), (), s32[]{:S(2)}) async-start(), calls=%async_computation.9 | async-start | bytes 9437184 | tf_op jit(solution)/shard_map/all_gather | solution.py:8
  801.2 490.9 %all-gather.13.cloned.1.call-start = ((), (), s32[]{:S(2)}) async-start(), calls=%async_computation.5 | async-start | bytes 71303168 | tf_op jit(solution)/shard_map/all_gather | solution.py:13
  899.8 5.7 copy-start.3
  923.7 441.7 %reduce-scatter.5.cloned.1.call-start = ((), (), s32[]{:S(2)}) async-start(), calls=%async_computation.6 | async-start | bytes 4718592 | tf_op jit(solution)/shard_map/reduce_scatter | solution.py:28
  1328.8 72.6 %all-gather.15.cloned.1.call-start = ((), (), s32[]{:S(2)}) async-start(), calls=%async_computation.7 | async-start | bytes 4718592 | tf_op jit(solution)/shard_map/all_gather | solution.py:29
  1401.4 30.7 %copy-start = (f32[4,512,2,512]{3,1,2,0:T(8,128)S(1)}, f32[4,512,2,512]{3,1,2,0:T(8,128)}, u32[]{:S(2)}) copy-start(f32[4,512,2,512]{3,1,2,0:T(8,128)} %select_dynamic-update-slice_fusion) | copy-start | bytes 25165828
  1401.4 30.7 %copy-start.1 = (f32[4,512,512]{1,0,2:T(4,128)S(1)}, f32[4,512,512]{1,0,2:T(4,128)}, u32[]{:S(2)}) copy-start(f32[4,512,512]{1,0,2:T(4,128)} %copy.59) | copy-start | bytes 12582916
Sparse Core Ops, SparseCore 0:
  95.8 53.2 all-gather.16
  222.3 368.2 all-gather.8
  624.0 36.4 reduce-scatter.2
  662.0 34.2 all-gather.10
  801.3 49.6 all-gather.18
  923.8 368.2 all-gather.12
  1328.9 36.4 reduce-scatter.4
  1367.1 34.2 all-gather.14
